TPU v7x, 32 devices: a whole 2x2x4 slice. The times are simulated.
32 devices in a mesh: ctx: 16 (over z, x, core), head: 2 (over y).
Axes of the slice: x: 2, y: 2, z: 4, core: 2. Of those that a mesh axis runs over, the one named last changes fastest.
Arguments:
- queries: bfloat16 [4096, 32, 128], P('ctx', 'head'), may hold values from -300 to 300
- key_rows: bfloat16 [4096, 4, 128], P('ctx', 'head'), may hold values from -6 to 6
- value_vectors: bfloat16 [4096, 4, 128], P('ctx', 'head'), may hold values from -6 to 6
- doc_ids: int32 [4096], replicated, may hold values from 0 to 2, never falling along the last dimension, each value on 1 to 1792 neighbouring positions
Outputs:
- attended: bfloat16 [4096, 32, 128], P(('ctx', 'head'))
Inputs may be any that keep to these rules, and one draw needn't show every extreme that they name: `doc_ids`: ids never fall along the pack and each prompt holds at most 1792 tokens.
All inputs are finite; a program needn't handle non-finite values.
Results may differ from a plain program's by a relative error of at most 0.008.
Values may be sent and summed in bfloat16 or wider, within the bound.
No kernel may reach another device: no remote copies, remote signals or barrier semaphores. Data moves between devices by JAX's collectives and lax.ppermute only.
A program may use at most 64 MiB of HBM per device.

v0:
```python
import jax
import jax.numpy as jnp
from jax import lax
from jax.sharding import PartitionSpec as P


def passed_along(block, axis, distance):
    devices = range(lax.axis_size(axis))
    route = [(i - distance, i) for i in devices if i - distance in devices]
    return lax.ppermute(block, axis, route)


def body(queries, key_rows, value_vectors, doc_ids):
    tok_len, heads_here, head_dim = queries.shape
    kv_heads = key_rows.shape[1]
    head_group = heads_here // kv_heads
    inv_root = head_dim ** (-0.5)
    cycle_size = lax.axis_size("ctx")
    reach_blocks = cycle_size // 2 - 1
    ctx_index = lax.axis_index("ctx")
    query_offset = ctx_index * tok_len
    own_doc = lax.dynamic_slice_in_dim(doc_ids, query_offset, tok_len, 0)
    own_pos = query_offset + jnp.arange(tok_len, dtype=jnp.int32)
    q_grouped = queries.reshape(tok_len, kv_heads, head_group, head_dim).transpose(1, 2, 0, 3)

    def attend(state, q_heads, query_doc, query_pos, key_block, value_block, key_start):
        key_len = key_block.shape[0]
        clamped = jnp.maximum(key_start, 0)
        key_doc = lax.dynamic_slice_in_dim(doc_ids, clamped, key_len, 0)
        key_pos = key_start + jnp.arange(key_len, dtype=jnp.int32)
        visible = (
            (query_doc[:, None] == key_doc[None, :])
            & (key_pos[None, :] <= query_pos[:, None])
            & (key_pos[None, :] >= 0)
        )
        key_major = key_block.transpose(1, 0, 2)
        value_major = value_block.transpose(1, 0, 2)

        def per_group(operand):
            q_group, k_group, v_group, run_max, run_sum, run_out = operand
            scores = (
                jnp.einsum("rtd,ud->rtu", q_group, k_group, preferred_element_type=jnp.float32)
                * inv_root
            )
            masked = jnp.where(visible[None], scores, -1e30)
            new_max = jnp.maximum(run_max, jnp.max(masked, axis=-1))
            weights = jnp.where(visible[None], jnp.exp(scores - new_max[..., None]), 0.0)
            rescale = jnp.exp(run_max - new_max)
            new_sum = run_sum * rescale + jnp.sum(weights, axis=-1)
            product = jnp.einsum(
                "rtu,ud->rtd",
                weights.astype(jnp.bfloat16),
                v_group,
                preferred_element_type=jnp.float32,
            )
            new_out = run_out * rescale[..., None] + product
            return (new_max, new_sum, new_out)

        return lax.map(per_group, (q_heads, key_major, value_major) + tuple(tuple(state)))

    state = attend(
        (
            jnp.full((kv_heads, head_group, tok_len), -1e30, jnp.float32),
            jnp.zeros((kv_heads, head_group, tok_len), jnp.float32),
            jnp.zeros((kv_heads, head_group, tok_len, head_dim), jnp.float32),
        ),
        q_grouped,
        own_doc,
        own_pos,
        key_rows,
        value_vectors,
        query_offset,
    )
    window_keys, window_values = (key_rows, value_vectors)
    covered = 1
    while covered < reach_blocks + 1:
        count = min(covered, reach_blocks + 1 - covered)
        arrived = passed_along((window_keys, window_values), "ctx", covered)
        window_keys = jnp.concatenate([arrived[0], window_keys], axis=0)
        window_values = jnp.concatenate([arrived[1], window_values], axis=0)
        covered = covered + count

    def window_turn(shard_num, carry):
        begin = (shard_num * tok_len).astype(jnp.int32)
        key_piece = lax.dynamic_slice_in_dim(window_keys, begin, tok_len, 0)
        value_piece = lax.dynamic_slice_in_dim(window_values, begin, tok_len, 0)
        return attend(
            carry,
            q_grouped,
            own_doc,
            own_pos,
            key_piece,
            value_piece,
            query_offset - (reach_blocks - shard_num) * tok_len,
        )

    state = lax.fori_loop(0, reach_blocks, window_turn, tuple(state))
    finished = (state[2] / state[1][..., None]).astype(jnp.bfloat16)
    merged = finished.transpose(2, 0, 1, 3).reshape(tok_len, heads_here, head_dim)
    return lax.all_to_all(merged, "head", split_axis=0, concat_axis=1, tiled=True)


def solution(mesh):
    placed = (P("ctx", "head", None), P("ctx", "head", None), P("ctx", "head", None), P())
    return jax.shard_map(
        body, mesh=mesh, in_specs=placed, out_specs=P(("ctx", "head"), None, None), check_vma=False
    )
```

profile of v0, /device:TPU:10, one launch (start us, length us, event | category | flops | bytes accessed | tf_op | source)
XLA Modules:
  0.0 105.9 jit_solution(14884595993120103621)
XLA Ops:
  0.0 1.7 %fusion.53 = (bf16[256,2,128]{2,0,1:T(8,128)(2,1)S(1)}, bf16[2,256,128]{2,1,0:T(8,128)(2,1)}, bf16[2,256,128]{2,1,0:T(8,128)(2,1)}, bf16[256,2,128]{2,0,1:T(8,128)(2,1)S(1)}) fusion(bf16[256,2,128]{2,1,0:T(2,128)(2,1)} %param.12, bf16[256,2,128]{2,1,0:T(2,128)(2,1)} %param.11), kind=kLoop, calls=%fused_computation.84 | loop fusion | bytes 786432 | tf_op args[2]
  1.7 1.9 %collective-permute-start = (bf16[256,2,128]{2,0,1:T(8,128)(2,1)S(1)}, bf16[256,2,128]{2,0,1:T(8,128)(2,1)S(1)}, u32[]{:S(2)}, u32[]{:S(2)}) collective-permute-start(bf16[256,2,128]{2,0,1:T(8,128)(2,1)S(1)} %get-tuple-element.557), channel_id=1, source_target_pairs={{0,2},{2,4},{4,6},{6,8},{8,10},{10,12},{12,14},{14,16},{16,18},{18... | collective-permute-start | bytes 393224 | tf_op jit(solution)/shard_map/ppermute | solution.py:10
  3.7 3.6 %collective-permute-start.3 = (bf16[256,2,128]{2,0,1:T(8,128)(2,1)S(1)}, bf16[256,2,128]{2,0,1:T(8,128)(2,1)S(1)}, u32[]{:S(2)}, u32[]{:S(2)}) collective-permute-start(bf16[256,2,128]{2,0,1:T(8,128)(2,1)S(1)} %get-tuple-element.550), channel_id=1, source_target_pairs={{0,2},{2,4},{4,6},{6,8},{8,10},{10,12},{12,14},{14,16},{16,18},{18... | collective-permute-start | bytes 393224 | tf_op jit(solution)/shard_map/ppermute | solution.py:10
  8.8 4.3 %collective-permute-start.1 = (bf16[512,2,128]{2,0,1:T(8,128)(2,1)}, bf16[512,2,128]{2,0,1:T(8,128)(2,1)}, u32[]{:S(2)}, u32[]{:S(2)}) collective-permute-start(bf16[512,2,128]{2,0,1:T(8,128)(2,1)} %pad_maximum_fusion.4), channel_id=1, source_target_pairs={{0,4},{2,6},{4,8},{6,10},{8,12},{10,14},{12,16},{14,18},{16,20},{1... | collective-permute-start | bytes 786440 | tf_op jit(solution)/shard_map/ppermute | solution.py:10
  13.9 2.5 %collective-permute-start.4 = (bf16[512,2,128]{2,0,1:T(8,128)(2,1)}, bf16[512,2,128]{2,0,1:T(8,128)(2,1)}, u32[]{:S(2)}, u32[]{:S(2)}) collective-permute-start(bf16[512,2,128]{2,0,1:T(8,128)(2,1)} %pad_maximum_fusion.5), channel_id=1, source_target_pairs={{0,4},{2,6},{4,8},{6,10},{8,12},{10,14},{12,16},{14,18},{16,20},{1... | collective-permute-start | bytes 786440 | tf_op jit(solution)/shard_map/ppermute | solution.py:10
  16.4 1.5 %copy.34 = bf16[256,16,128]{2,0,1:T(8,128)(2,1)S(1)} copy(bf16[256,16,128]{2,1,0:T(8,128)(2,1)} %param.10) | data formatting | bytes 2097152 | tf_op args[0]
  20.1 1.8 %pad_maximum_fusion.2 = bf16[1024,2,128]{2,0,1:T(8,128)(2,1)} fusion(bf16[256,2,128]{2,0,1:T(8,128)(2,1)S(1)} %get-tuple-element.557, bf16[256,2,128]{2,0,1:T(8,128)(2,1)} %copy-done.3, bf16[512,2,128]{2,0,1:T(8,128)(2,1)} %collective-permute-done.1), kind=kLoop, calls=%fused_computation.76 | loop fusion | flops 1572864 | bytes 1048576 | tf_op jit(solution)/shard_map/concatenate | solution.py:79
  22.0 3.5 %collective-permute-start.2 = (bf16[1024,2,128]{2,0,1:T(8,128)(2,1)}, bf16[1024,2,128]{2,0,1:T(8,128)(2,1)}, u32[]{:S(2)}, u32[]{:S(2)}) collective-permute-start(bf16[1024,2,128]{2,0,1:T(8,128)(2,1)} %pad_maximum_fusion.2), channel_id=1, source_target_pairs={{0,8},{2,10},{4,12},{6,14},{8,16},{10,18},{12,20},{14,22},{16,24},... | collective-permute-start | bytes 1572872 | tf_op jit(solution)/shard_map/ppermute | solution.py:10
  25.5 1.9 %pad_maximum_fusion.3 = bf16[1024,2,128]{2,0,1:T(8,128)(2,1)} fusion(bf16[256,2,128]{2,0,1:T(8,128)(2,1)S(1)} %get-tuple-element.550, bf16[256,2,128]{2,0,1:T(8,128)(2,1)} %copy-done.1, bf16[512,2,128]{2,0,1:T(8,128)(2,1)} %collective-permute-done.4), kind=kLoop, calls=%fused_computation.77 | loop fusion | flops 1572864 | bytes 1048576 | tf_op jit(solution)/shard_map/concatenate | solution.py:80
  27.3 3.3 %collective-permute-start.5 = (bf16[1024,2,128]{2,0,1:T(8,128)(2,1)}, bf16[1024,2,128]{2,0,1:T(8,128)(2,1)}, u32[]{:S(2)}, u32[]{:S(2)}) collective-permute-start(bf16[1024,2,128]{2,0,1:T(8,128)(2,1)} %pad_maximum_fusion.3), channel_id=1, source_target_pairs={{0,8},{2,10},{4,12},{6,14},{8,16},{10,18},{12,20},{14,22},{16,24},... | collective-permute-start | bytes 1572872 | tf_op jit(solution)/shard_map/ppermute | solution.py:10
  30.7 5.7 %while.66 = (s32[]{:T(128)}, f32[2,8,256]{2,1,0:T(8,128)S(1)}, f32[2,8,256]{2,1,0:T(8,128)S(1)}, f32[2,8,256,128]{3,2,1,0:T(8,128)S(1)}, bf16[2,8,256,128]{3,2,1...) while((s32[]{:T(128)}, f32[2,8,256]{2,1,0:T(8,128)S(1)}, ...), condition=%wide.region_3.4_spmd.clone, body=%wide.region_0.3_spmd.clone.sunk | while | flops 274737152 | bytes 8885661 | solution.py:59
  36.4 2.6 %collective-permute-done.2 = bf16[1024,2,128]{2,0,1:T(8,128)(2,1)} collective-permute-done((bf16[1024,2,128]{2,0,1:T(8,128)(2,1)}, bf16[1024,2,128]{2,0,1:T(8,128)(2,1)}, u32[]{:S(2)}, u32[]{:S(2)}) %collective-permute-start.2) | collective-permute-done | bytes 524320 | tf_op jit(solution)/shard_map/ppermute | solution.py:10
  39.0 2.3 %pad_maximum_fusion = bf16[2048,2,128]{2,0,1:T(8,128)(2,1)} fusion(bf16[256,2,128]{2,0,1:T(8,128)(2,1)} %copy-done, bf16[256,2,128]{2,0,1:T(8,128)(2,1)} %copy-done.3, bf16[512,2,128]{2,0,1:T(8,128)(2,1)} %collective-permute-done.1, bf16[1024,2,128]{2,0,1:T(8,128)(2,1)} %collective-permute-done.2), kind=kLoop, calls=%fused_computation.72 | loop fusion | flops 4194304 | bytes 2097152 | tf_op jit(solution)/shard_map/concatenate | solution.py:79
  41.3 5.3 %collective-permute-done.5 = bf16[1024,2,128]{2,0,1:T(8,128)(2,1)} collective-permute-done((bf16[1024,2,128]{2,0,1:T(8,128)(2,1)}, bf16[1024,2,128]{2,0,1:T(8,128)(2,1)}, u32[]{:S(2)}, u32[]{:S(2)}) %collective-permute-start.5) | collective-permute-done | bytes 524320 | tf_op jit(solution)/shard_map/ppermute | solution.py:10
  46.6 2.2 %pad_maximum_fusion.1 = bf16[2048,2,128]{2,0,1:T(8,128)(2,1)} fusion(bf16[256,2,128]{2,0,1:T(8,128)(2,1)S(1)} %get-tuple-element.550, bf16[256,2,128]{2,0,1:T(8,128)(2,1)S(1)} %copy-done.2, bf16[512,2,128]{2,0,1:T(8,128)(2,1)} %collective-permute-done.4, bf16[1024,2,128]{2,0,1:T(8,128)(2,1)} %collective-permute-done.5), kind=kLoop, calls=%fused_computation.73 | loop fusion | flops 4194304 | bytes 2097152 | tf_op jit(solution)/shard_map/concatenate | solution.py:80
  48.8 41.6 %while.68 = (s32[]{:T(128)}, f32[2,8,256]{2,1,0:T(8,128)S(1)}, f32[2,8,256]{2,1,0:T(8,128)S(1)}, f32[2,8,256,128]{3,2,1,0:T(8,128)S(1)}, bf16[2048,2,128]{2,0,1:...) while((s32[]{:T(128)}, f32[2,8,256]{2,1,0:T(8,128)S(1)}, ...), condition=%wide.region_9.10_spmd.clone.clone, body=%wide.region_4.9_spmd.clone.clone.sunk | while | flops 274998272 | bytes 12061712 | solution.py:97
  50.6 4.1 %while.69 = (s32[]{:T(128)}, f32[2,8,256]{2,1,0:T(8,128)S(1)}, f32[2,8,256]{2,1,0:T(8,128)S(1)}, f32[2,8,256,128]{3,2,1,0:T(8,128)S(1)}, bf16[2,8,256,128]{3,2,1...) while((s32[]{:T(128)}, f32[2,8,256]{2,1,0:T(8,128)S(1)}, ...), condition=%wide.region_8.8_spmd.clone.clone, body=%wide.region_5.7_spmd.clone.clone.sunk | while | flops 274997248 | bytes 11532689 | solution.py:59
  56.5 4.1 %while.69 = (s32[]{:T(128)}, f32[2,8,256]{2,1,0:T(8,128)S(1)}, f32[2,8,256]{2,1,0:T(8,128)S(1)}, f32[2,8,256,128]{3,2,1,0:T(8,128)S(1)}, bf16[2,8,256,128]{3,2,1...) while((s32[]{:T(128)}, f32[2,8,256]{2,1,0:T(8,128)S(1)}, ...), condition=%wide.region_8.8_spmd.clone.clone, body=%wide.region_5.7_spmd.clone.clone.sunk | while | flops 274997248 | bytes 11532689 | solution.py:59
  62.5 4.1 %while.69 = (s32[]{:T(128)}, f32[2,8,256]{2,1,0:T(8,128)S(1)}, f32[2,8,256]{2,1,0:T(8,128)S(1)}, f32[2,8,256,128]{3,2,1,0:T(8,128)S(1)}, bf16[2,8,256,128]{3,2,1...) while((s32[]{:T(128)}, f32[2,8,256]{2,1,0:T(8,128)S(1)}, ...), condition=%wide.region_8.8_spmd.clone.clone, body=%wide.region_5.7_spmd.clone.clone.sunk | while | flops 274997248 | bytes 11532689 | solution.py:59
  68.4 4.1 %while.69 = (s32[]{:T(128)}, f32[2,8,256]{2,1,0:T(8,128)S(1)}, f32[2,8,256]{2,1,0:T(8,128)S(1)}, f32[2,8,256,128]{3,2,1,0:T(8,128)S(1)}, bf16[2,8,256,128]{3,2,1...) while((s32[]{:T(128)}, f32[2,8,256]{2,1,0:T(8,128)S(1)}, ...), condition=%wide.region_8.8_spmd.clone.clone, body=%wide.region_5.7_spmd.clone.clone.sunk | while | flops 274997248 | bytes 11532689 | solution.py:59
  74.4 4.1 %while.69 = (s32[]{:T(128)}, f32[2,8,256]{2,1,0:T(8,128)S(1)}, f32[2,8,256]{2,1,0:T(8,128)S(1)}, f32[2,8,256,128]{3,2,1,0:T(8,128)S(1)}, bf16[2,8,256,128]{3,2,1...) while((s32[]{:T(128)}, f32[2,8,256]{2,1,0:T(8,128)S(1)}, ...), condition=%wide.region_8.8_spmd.clone.clone, body=%wide.region_5.7_spmd.clone.clone.sunk | while | flops 274997248 | bytes 11532689 | solution.py:59
  80.3 4.1 %while.69 = (s32[]{:T(128)}, f32[2,8,256]{2,1,0:T(8,128)S(1)}, f32[2,8,256]{2,1,0:T(8,128)S(1)}, f32[2,8,256,128]{3,2,1,0:T(8,128)S(1)}, bf16[2,8,256,128]{3,2,1...) while((s32[]{:T(128)}, f32[2,8,256]{2,1,0:T(8,128)S(1)}, ...), condition=%wide.region_8.8_spmd.clone.clone, body=%wide.region_5.7_spmd.clone.clone.sunk | while | flops 274997248 | bytes 11532689 | solution.py:59
  86.3 4.1 %while.69 = (s32[]{:T(128)}, f32[2,8,256]{2,1,0:T(8,128)S(1)}, f32[2,8,256]{2,1,0:T(8,128)S(1)}, f32[2,8,256,128]{3,2,1,0:T(8,128)S(1)}, bf16[2,8,256,128]{3,2,1...) while((s32[]{:T(128)}, f32[2,8,256]{2,1,0:T(8,128)S(1)}, ...), condition=%wide.region_8.8_spmd.clone.clone, body=%wide.region_5.7_spmd.clone.clone.sunk | while | flops 274997248 | bytes 11532689 | solution.py:59
  91.8 12.9 %all_to_all.18 = bf16[256,16,128]{2,1,0:T(8,128)(2,1)S(1)} all-to-all(bf16[256,16,128]{2,1,0:T(8,128)(2,1)S(1)} %bitcast.122), channel_id=1, replica_groups=mesh['ctx'=16,'head'=2] {'head'}, dimensions={0} | all-to-all | bytes 2097152 | tf_op jit(solution)/shard_map/all_to_all | solution.py:100
  (165 shorter events, 53.0 us)
Async XLA Ops:
  1.7 20.2 %copy-start = (bf16[256,2,128]{2,0,1:T(8,128)(2,1)}, bf16[256,2,128]{2,0,1:T(8,128)(2,1)S(1)}, u32[]{:S(2)}) copy-start(bf16[256,2,128]{2,0,1:T(8,128)(2,1)S(1)} %get-tuple-element.557) | copy-start | bytes 393220
  1.7 6.3 %collective-permute-start = (bf16[256,2,128]{2,0,1:T(8,128)(2,1)S(1)}, bf16[256,2,128]{2,0,1:T(8,128)(2,1)S(1)}, u32[]{:S(2)}, u32[]{:S(2)}) collective-permute-start(bf16[256,2,128]{2,0,1:T(8,128)(2,1)S(1)} %get-tuple-element.557), channel_id=1, source_target_pairs={{0,2},{2,4},{4,6},{6,8},{8,10},{10,12},{12,14},{14,16},{16,18},{18... | collective-permute-start | bytes 393224 | tf_op jit(solution)/shard_map/ppermute | solution.py:10
  3.7 9.5 %collective-permute-start.3 = (bf16[256,2,128]{2,0,1:T(8,128)(2,1)S(1)}, bf16[256,2,128]{2,0,1:T(8,128)(2,1)S(1)}, u32[]{:S(2)}, u32[]{:S(2)}) collective-permute-start(bf16[256,2,128]{2,0,1:T(8,128)(2,1)S(1)} %get-tuple-element.550), channel_id=1, source_target_pairs={{0,2},{2,4},{4,6},{6,8},{8,10},{10,12},{12,14},{14,16},{16,18},{18... | collective-permute-start | bytes 393224 | tf_op jit(solution)/shard_map/ppermute | solution.py:10
  8.0 8.4 %copy-start.3 = (bf16[256,2,128]{2,0,1:T(8,128)(2,1)}, bf16[256,2,128]{2,0,1:T(8,128)(2,1)S(1)}, u32[]{:S(2)}) copy-start(bf16[256,2,128]{2,0,1:T(8,128)(2,1)S(1)} %collective-permute-done) | copy-start | bytes 393220
  8.8 11.4 %collective-permute-start.1 = (bf16[512,2,128]{2,0,1:T(8,128)(2,1)}, bf16[512,2,128]{2,0,1:T(8,128)(2,1)}, u32[]{:S(2)}, u32[]{:S(2)}) collective-permute-start(bf16[512,2,128]{2,0,1:T(8,128)(2,1)} %pad_maximum_fusion.4), channel_id=1, source_target_pairs={{0,4},{2,6},{4,8},{6,10},{8,12},{10,14},{12,16},{14,18},{16,20},{1... | collective-permute-start | bytes 786440 | tf_op jit(solution)/shard_map/ppermute | solution.py:10
  13.1 3.3 %copy-start.1 = (bf16[256,2,128]{2,0,1:T(8,128)(2,1)}, bf16[256,2,128]{2,0,1:T(8,128)(2,1)S(1)}, u32[]{:S(2)}) copy-start(bf16[256,2,128]{2,0,1:T(8,128)(2,1)S(1)} %collective-permute-done.3) | copy-start | bytes 393220
  13.9 11.6 %collective-permute-start.4 = (bf16[512,2,128]{2,0,1:T(8,128)(2,1)}, bf16[512,2,128]{2,0,1:T(8,128)(2,1)}, u32[]{:S(2)}, u32[]{:S(2)}) collective-permute-start(bf16[512,2,128]{2,0,1:T(8,128)(2,1)} %pad_maximum_fusion.5), channel_id=1, source_target_pairs={{0,4},{2,6},{4,8},{6,10},{8,12},{10,14},{12,16},{14,18},{16,20},{1... | collective-permute-start | bytes 786440 | tf_op jit(solution)/shard_map/ppermute | solution.py:10
  22.0 17.0 %collective-permute-start.2 = (bf16[1024,2,128]{2,0,1:T(8,128)(2,1)}, bf16[1024,2,128]{2,0,1:T(8,128)(2,1)}, u32[]{:S(2)}, u32[]{:S(2)}) collective-permute-start(bf16[1024,2,128]{2,0,1:T(8,128)(2,1)} %pad_maximum_fusion.2), channel_id=1, source_target_pairs={{0,8},{2,10},{4,12},{6,14},{8,16},{10,18},{12,20},{14,22},{16,24},... | collective-permute-start | bytes 1572872 | tf_op jit(solution)/shard_map/ppermute | solution.py:10
  27.3 19.3 %collective-permute-start.5 = (bf16[1024,2,128]{2,0,1:T(8,128)(2,1)}, bf16[1024,2,128]{2,0,1:T(8,128)(2,1)}, u32[]{:S(2)}, u32[]{:S(2)}) collective-permute-start(bf16[1024,2,128]{2,0,1:T(8,128)(2,1)} %pad_maximum_fusion.3), channel_id=1, source_target_pairs={{0,8},{2,10},{4,12},{6,14},{8,16},{10,18},{12,20},{14,22},{16,24},... | collective-permute-start | bytes 1572872 | tf_op jit(solution)/shard_map/ppermute | solution.py:10
  30.8 1.9 %copy-start.4 = (bf16[2,256,128]{2,1,0:T(8,128)(2,1)S(1)}, bf16[2,256,128]{2,1,0:T(8,128)(2,1)}, u32[]{:S(2)}) copy-start(bf16[2,256,128]{2,1,0:T(8,128)(2,1)} %get-tuple-element.891) | copy-start | bytes 393220 | tf_op jit(solution)/shard_map/while
  33.7 1.9 %copy-start.4 = (bf16[2,256,128]{2,1,0:T(8,128)(2,1)S(1)}, bf16[2,256,128]{2,1,0:T(8,128)(2,1)}, u32[]{:S(2)}) copy-start(bf16[2,256,128]{2,1,0:T(8,128)(2,1)} %get-tuple-element.891) | copy-start | bytes 393220 | tf_op jit(solution)/shard_map/while
  36.4 10.2 %copy-start.2 = (bf16[256,2,128]{2,0,1:T(8,128)(2,1)S(1)}, bf16[256,2,128]{2,0,1:T(8,128)(2,1)}, u32[]{:S(2)}) copy-start(bf16[256,2,128]{2,0,1:T(8,128)(2,1)} %copy-done.1) | copy-start | bytes 393220
where the time goes:
time: 107 us; the launch traced here: 106 us
  matrix products  22.1 us (21%)
  other arithmetic  20.8 us (19%)
  local copies, waits for them, and re-layouts  19.4 us (18%)
  starting transfers between devices  19.1 us (18%)
  blocking collectives  12.9 us (12%)
  waiting for transfers between devices  10.1 us (9%)
  loops' own time  1.35 us (1%)
    ppermute x6, starting transfers between devices, passed_along(): return lax.ppermute(block, axis, route)  19.1 us
    all_to_all x1, blocking collectives, body(): lax.all_to_all(merged, 'head', split_axis=0, concat_axis=1, tiled=True)  12.9 us
    dot_general x16, matrix products, per_group(): jnp.einsum('rtu,ud->rtd', weights.astype(jnp.bfloat16), v_group, preferre...  12.8 us
    ppermute x6, waiting for transfers between devices, passed_along(): return lax.ppermute(block, axis, route)  10.1 us
    dot_general x16, matrix products, per_group(): jnp.einsum('rtd,ud->rtu', q_group, k_group, preferred_element_type=jnp.fl...  9.26 us
    reduce_sum x16, other arithmetic, per_group(): new_sum = run_sum * rescale + jnp.sum(weights, axis=-1)  7.09 us
    transpose x7, local copies, waits for them, and re-layouts, attend(): value_major = value_block.transpose(1, 0, 2)  6.97 us
    dynamic_slice x7, local copies, waits for them, and re-layouts, attend(): key_doc = lax.dynamic_slice_in_dim(doc_ids, clamped, key_len, 0)  5.45 us
  transfers between devices with their start and end apart: 6, of which 4 were waited for; matrix products, arithmetic and copies ran while one was open for 15% of the time, Pallas kernels for 0%

commit v1 on v0

v1 whole, which is shorter than its diff:
```python
import functools
import math

import jax
import jax.numpy as jnp
from jax import lax
from jax.experimental import pallas as pl
from jax.experimental.pallas import tpu as pltpu
from jax.sharding import PartitionSpec as P


QUAD = 4
CHUNK = 512
LANES = 128
NEAR_HOPS = 3
HIDDEN = -1e30
FAR_SLOT = 5
EMPTY = -(1 << 30)
SMALL = 64
CEILING = 2.0**100
FLOOR = 2.0**-100


def shifted(block, distance):
    n = lax.axis_size("ctx")
    return lax.ppermute(block, "ctx", [(i, (i + distance) % n) for i in range(n)])


def swapped(block, bit):
    n = lax.axis_size("ctx")
    return lax.ppermute(block, "ctx", [(i, i ^ bit) for i in range(n)])


def crossed(block):
    return lax.ppermute(block, "head", [(0, 1), (1, 0)])


def in_vmem(count):
    return [pl.BlockSpec(memory_space=pltpu.VMEM)] * count


def hops_needed():
    reach = lax.axis_size("ctx") // 2 - 1
    return -(-reach // QUAD)


def near(*arrays):
    if hops_needed() > NEAR_HOPS:
        return list(arrays)
    return [pltpu.with_memory_space_constraint(a, pltpu.VMEM) for a in arrays]


def near_shape(shape, dtype):
    if hops_needed() > NEAR_HOPS:
        return jax.ShapeDtypeStruct(shape, dtype)
    return pltpu.VMEM(shape, dtype)


def pack_kernel(k_ref, v_ref, *refs):
    *outs, k_wide, v_wide = refs
    heads = len(outs)
    tok = k_ref.shape[0] // heads
    k_wide[...] = k_ref[...].astype(jnp.float32)
    v_wide[...] = v_ref[...].astype(jnp.float32)
    for g, out in enumerate(outs):
        out[0:tok, :] = k_wide[pl.ds(g, tok, heads), :].astype(jnp.bfloat16)
        out[tok : 2 * tok, :] = v_wide[pl.ds(g, tok, heads), :].astype(jnp.bfloat16)


def packed(key_rows, value_vectors):
    tok, kv_heads, dim = key_rows.shape
    flat = (tok * kv_heads, dim)
    return pl.pallas_call(
        pack_kernel,
        out_shape=[near_shape((2 * tok, dim), jnp.bfloat16)] * kv_heads,
        in_specs=in_vmem(2),
        out_specs=in_vmem(kv_heads),
        scratch_shapes=[pltpu.VMEM(flat, jnp.float32)] * 2,
        name="pack",
    )(key_rows.reshape(flat), value_vectors.reshape(flat))


def take(out_ref, at, choices):
    for wanted, ref in choices:

        def copy(ref=ref):
            out_ref[at : at + ref.shape[0], :] = ref[...]

        if wanted is None:
            copy()
        else:
            pl.when(wanted)(copy)


def joined(first, second):
    arrays = [array for _, array in first + second]
    size, dim = arrays[0].shape

    def kernel(*refs):
        *ins, out_ref = refs
        me = lax.axis_index("ctx")
        wanted = [None if test is None else test(me) for test, _ in first + second]
        choices = list(zip(wanted, ins))
        take(out_ref, 0, choices[: len(first)])
        take(out_ref, size, choices[len(first) :])

    return pl.pallas_call(
        kernel,
        out_shape=near_shape((2 * size, dim), jnp.bfloat16),
        in_specs=in_vmem(len(arrays)),
        out_specs=pl.BlockSpec(memory_space=pltpu.VMEM),
        name="join",
    )(*near(*arrays))


def upper(me):
    return me & 1 == 1


def lower(me):
    return me & 1 == 0


def right(me):
    return me & 2 == 2


def left(me):
    return me & 2 == 0


def both(test, other):
    return lambda me: test(me) & other(me)


def chosen(test, yes, no):
    return jnp.where(test(lax.axis_index("ctx")), yes, no)


def gathered(own, hops, across_first):
    arrays = [own]
    line = own

    def twin(first, second):
        pair = joined(first, second)
        return [pair, swapped(pair, 1)]

    if across_first:
        beside = swapped(own, 2)
        line = shifted(own, QUAD)
        wide = shifted(chosen(left, beside, line), QUAD)
        back = shifted(line, QUAD)
        arrays += twin([(None, line)], [(right, beside), (left, wide)])
        across = swapped(chosen(left, line, wide), 2)
        last = [(lower, own), (both(upper, right), wide), (both(upper, left), back)]
    else:
        for _ in range(1, hops):
            line = shifted(line, QUAD)
            across = swapped(line, 2)
            arrays += twin([(None, line)], [(None, across)])
        line = shifted(line, QUAD)
        across = swapped(chosen(left, own, line), 2)
        last = [(lower, own), (upper, line)]
    return arrays + [across, twin(last, [(None, across)])[1]]


def slot_table(me, hops, across_first):
    near_hop = jnp.where(right(me), 0, 1)
    far_hop = jnp.where(right(me), 1 if across_first else 0, hops)
    table = [(0, 0, 0, 0)]
    for hop in range(1, hops):
        a = 2 * hop - 1
        beside = near_hop if across_first else hop
        table += [(a, 0, 0, hop), (a, 1, 2, beside)]
        table += [(a + 1, 0, 1, hop), (a + 1, 1, 3, beside)]
    a = 2 * hops - 1
    table += [(a, 0, 2, far_hop), (a + 1, 0, 1, jnp.where(upper(me), 0, hops))]
    return table + [(a + 1, 1, 3, far_hop)]


class Rows:
    def __init__(self, docs_ref, q_ref, group, start_ref, offset, tok):
        self.q_ref, self.group, self.start_ref, self.tok = q_ref, group, start_ref, tok
        count, _, self.dim = q_ref.shape
        self.chunks = count * group // CHUNK
        self.me = lax.axis_index("ctx")
        self.base = self.me * self.tok + offset
        docs = docs_ref[...]
        bound_1 = jnp.sum((docs < 1).astype(jnp.int32))
        bound_2 = jnp.sum((docs < 2).astype(jnp.int32))

        def start_of(pos):
            return jnp.where(pos >= bound_2, bound_2, jnp.where(pos >= bound_1, bound_1, 0))

        self.first_start = start_of(self.base)
        for r in range(self.chunks):
            start_ref[pl.ds(r * CHUNK, CHUNK)] = start_of(self.positions(r * CHUNK, CHUNK))

    def positions(self, row, size):
        rows = lax.broadcasted_iota(jnp.int32, (size, LANES), 0)
        return rows // self.group + (self.base + row // self.group)

    def low_of(self, turn, hop):
        block = (self.me ^ turn) - QUAD * hop
        low = block * self.tok
        live = (block >= 0) & (block < self.me) & (low + self.tok > self.first_start)
        return jnp.where(live, low, EMPTY)

    def scores(self, g, keys, row, size):
        first = row // self.group
        q = self.q_ref[pl.ds(first, size // self.group), pl.ds(g * self.group, self.group)]
        return lax.dot_general(
            q.reshape(size, self.dim),
            keys,
            (((1,), (1,)), ((), ())),
            preferred_element_type=jnp.float32,
        )

    def masked(self, fill, values, low, own, row, size):
        parts = []
        for h in range(0, self.tok, LANES):
            key = lax.broadcasted_iota(jnp.int32, (size, LANES), 1) + (low + h)
            seen = key >= self.start_ref[pl.ds(row, size)]
            if own:
                seen = seen & (key <= self.positions(row, size))
            parts.append(jnp.where(seen, values[:, h : h + LANES], fill))
        return jnp.concatenate(parts, axis=1)


def gained(weights, values):
    both = jnp.concatenate([values, jnp.ones_like(values)], axis=1)
    return lax.dot_general(
        weights, both, (((1,), (0,)), ((), ())), preferred_element_type=jnp.float32
    )


def stream(rows, scale, p_buf, items):
    def weigh(n):
        g, keys, _, low, own, row, _ = items[n]
        weights = jnp.exp2(rows.scores(g, keys(), row, CHUNK) * scale)
        weights = rows.masked(0.0, weights, low, own, row, CHUNK)
        p_buf[n % 2] = weights.astype(jnp.bfloat16)

    weigh(0)
    for n, (_, _, values, _, _, _, keep) in enumerate(items):
        if n + 1 < len(items):
            weigh(n + 1)
        keep(gained(p_buf[n % 2], values()))


def halves_of(ref, part, tok):
    first = 2 * tok * part
    return (lambda: ref[first : first + tok]), (lambda: ref[first + tok : first + 2 * tok])


def fetch_kernel(q_hbm, docs_ref, *refs):
    *q_outs, docs_out, sem = refs
    half, group, _ = q_outs[0].shape
    side = lax.axis_index("head")
    tokens = pl.ds(pl.multiple_of((1 - side) * half, half), half)
    copies = []
    for g, q_out in enumerate(q_outs):
        part = q_hbm.at[tokens, pl.ds(g * group, group)]
        copies.append(pltpu.make_async_copy(part, q_out, sem.at[g]))
        copies[g].start()
    docs_out[...] = docs_ref[...]
    for copy in copies:
        copy.wait()


def attend_kernel(scale, hops, groups, group, home, *refs):
    refs = list(refs)
    heads = len(groups)
    q_in = refs.pop(0)
    docs_ref = refs.pop(0)
    arrays = [[refs.pop(0) for _ in range(2 * hops + 1)] for _ in groups]
    out_ref, acc_ref, start_ref, top_ref, p_buf = refs[:5]
    side = lax.axis_index("head")
    if home:
        q_ref, piece_ref, sem = refs[5:]
        half, _, dim = q_ref.shape
        offset = pl.multiple_of(side * half, half)
        q_copy = pltpu.make_async_copy(q_in.at[pl.ds(offset, half)], q_ref, sem.at[0])
        q_copy.start()
    else:
        q_ref = q_in
        half, _, dim = q_ref.shape
        offset = pl.multiple_of((1 - side) * half, half)
    tok = 2 * half
    size = half * group
    rows = Rows(docs_ref, q_ref, group, start_ref, offset, tok)
    tables, lows = [], []
    for _, across_first in groups:
        tables.append(slot_table(rows.me, hops, across_first))
        lows.append([rows.low_of(turn, hop) for _, _, turn, hop in tables[-1]])
        lows[-1][0] = rows.me * tok
    if home:
        q_copy.wait()
    slots = range(len(tables[0]))
    chunks = size // CHUNK

    def item(n, s, row):
        keys, values = halves_of(arrays[n][tables[n][s][0]], tables[n][s][1], tok)

        def keep(gain):
            at = pl.ds(n * size + row, CHUNK)
            acc_ref[at] = gain if s == 0 else acc_ref[at] + gain

        return (n, keys, values, lows[n][s], s == 0, row, keep)

    if hops <= NEAR_HOPS:

        def run(some):
            order = [(n, s, r * CHUNK) for n in range(heads) for s in some for r in range(chunks)]
            stream(rows, scale, p_buf, [item(*at) for at in order])

        close, distant = slots[1:FAR_SLOT], slots[FAR_SLOT:]

        def held(some):
            return functools.reduce(jnp.maximum, [low[s] for low in lows for s in some]) >= 0

        every = held(close) & held(distant)
        pl.when(every)(lambda: run(slots))

        @pl.when(jnp.logical_not(every))
        def _():
            run(slots[:1])
            pl.when(held(close))(lambda: run(close))
            pl.when(held(distant))(lambda: run(distant))

    else:

        def step(r, carry):
            row = pl.multiple_of(r * CHUNK, CHUNK)
            stream(rows, scale, p_buf, [item(n, s, row) for n in range(heads) for s in slots])
            return carry

        lax.fori_loop(0, chunks, step, 0)

    total = acc_ref[:, dim:]
    bad = jnp.max(jnp.where((total < CEILING) & (total > FLOOR), 0.0, 1.0))

    @pl.when(bad > 0.0)
    def _():
        top_ref[...] = jnp.full_like(top_ref, HIDDEN)
        acc_ref[...] = jnp.zeros_like(acc_ref)
        for n in range(heads):
            for s in slots:
                keys, values = halves_of(arrays[n][tables[n][s][0]], tables[n][s][1], tok)

                def careful(i, carry, keys=keys, values=values, n=n, s=s):
                    row = pl.multiple_of(i * SMALL, SMALL)
                    at = pl.ds(pl.multiple_of(n * size + row, SMALL), SMALL)
                    scores = rows.scores(n, keys(), row, SMALL) * scale
                    scores = rows.masked(HIDDEN, scores, lows[n][s], s == 0, row, SMALL)
                    old = top_ref[at]
                    top = jnp.maximum(old, jnp.max(scores, axis=1, keepdims=True))
                    weights = jnp.exp2(scores - top[:, 0:1]).astype(jnp.bfloat16)
                    fade = jnp.exp2(old - top)
                    fade = jnp.concatenate([fade, fade], axis=1)
                    acc_ref[at] = acc_ref[at] * fade + gained(weights, values())
                    top_ref[at] = top
                    return carry

                @pl.when(lows[n][s] >= 0)
                def _(careful=careful):
                    lax.fori_loop(0, size // SMALL, careful, 0)

    span = CHUNK // group
    for n in range(heads):
        for r in range(chunks):
            gain = acc_ref[n * size + r * CHUNK : n * size + (r + 1) * CHUNK]
            done = gain[:, :dim] * pl.reciprocal(gain[:, dim:], approx=False)
            done = done.reshape(span, group, dim).astype(jnp.bfloat16)
            to = piece_ref.at[n] if home else out_ref
            to[r * span : (r + 1) * span] = done
        if home:
            start_put(piece_ref.at[n], out_ref, groups[n][0], side, sem.at[n])
    if home:
        for n in range(heads):
            start_put(piece_ref.at[n], out_ref, groups[n][0], side, sem.at[n], wait=True)


def start_put(piece, out_hbm, g, half, sem, wait=False):
    group, heads = piece.shape[1], out_hbm.shape[1]
    first = pl.multiple_of(half * (heads // 2) + g * group, group)
    copy = pltpu.make_async_copy(piece, out_hbm.at[:, pl.ds(first, group)], sem)
    if wait:
        copy.wait()
    else:
        copy.start()


def place_kernel(out_in, *refs):
    *pieces, out_ref, sem = refs
    half = 1 - lax.axis_index("head")
    for wait in (False, True):
        for g, piece in enumerate(pieces):
            start_put(piece, out_ref, g, half, sem.at[g], wait)


def on_chip(kernel, out_shape, out_specs, scratch, in_hbm, *operands, aliases=None):
    anywhere = pl.BlockSpec(memory_space=pl.ANY)
    return pl.pallas_call(
        kernel,
        out_shape=out_shape,
        in_specs=[anywhere] * len(in_hbm) + in_vmem(len(operands)),
        out_specs=out_specs,
        scratch_shapes=scratch,
        input_output_aliases=aliases or {},
    )(*in_hbm, *near(*operands))


def body(queries, key_rows, value_vectors, doc_ids):
    tok, heads_here, dim = queries.shape
    kv_heads = key_rows.shape[1]
    group = heads_here // kv_heads
    hops = hops_needed()
    scale = dim ** (-0.5) * math.log2(math.e)
    docs = doc_ids.reshape(-1, LANES)
    half = tok // 2
    output = jax.ShapeDtypeStruct((half, 2 * heads_here, dim), jnp.bfloat16)
    anywhere = pl.BlockSpec(memory_space=pl.ANY)

    own = packed(key_rows, value_vectors)
    piece = near_shape((half, group, dim), jnp.bfloat16)
    *q_away, docs = on_chip(
        fetch_kernel,
        [piece] * kv_heads + [near_shape(docs.shape, docs.dtype)],
        in_vmem(kv_heads + 1),
        [pltpu.SemaphoreType.DMA((kv_heads,))],
        [queries],
        docs,
    )

    def scratch(heads):
        rows = half * group
        return [
            pltpu.VMEM((heads * rows, 2 * dim), jnp.float32),
            pltpu.VMEM((rows, LANES), jnp.int32),
            pltpu.VMEM((heads * rows, dim), jnp.float32),
            pltpu.VMEM((2, CHUNK, tok), jnp.bfloat16),
        ]

    groups, windows, others = [], [], []
    for g in range(kv_heads):
        groups.append((g, hops == 2 and g % 2 == 1))
        windows.append(gathered(own[g], hops, groups[g][1]))
        away = on_chip(
            functools.partial(attend_kernel, scale, hops, groups[g : g + 1], group, False),
            piece,
            pl.BlockSpec(memory_space=pltpu.VMEM),
            scratch(1),
            [],
            q_away[g], docs, *windows[g],
        )
        others.append(crossed(away))
    result = on_chip(
        functools.partial(attend_kernel, scale, hops, groups, group, True),
        output,
        anywhere,
        scratch(kv_heads)
        + [
            pltpu.VMEM((half, heads_here, dim), jnp.bfloat16),
            pltpu.VMEM((kv_heads, half, group, dim), jnp.bfloat16),
            pltpu.SemaphoreType.DMA((kv_heads,)),
        ],
        [queries],
        docs, *[array for window in windows for array in window],
    )
    return on_chip(
        place_kernel, output, anywhere, [pltpu.SemaphoreType.DMA((kv_heads,))],
        [result], *others, aliases={0: 0},
    )


def solution(mesh):
    placed = (P("ctx", "head", None), P("ctx", "head", None), P("ctx", "head", None), P())

    return jax.shard_map(
        body, mesh=mesh, in_specs=placed, out_specs=P(("ctx", "head"), None, None), check_vma=False
    )
```

time: 107 us -> 265 us (2.48)
  the two profiles are of different devices: /device:TPU:10 before, /device:TPU:28 now
where the time goes in v1:
time: 265 us
  Pallas kernels  129 us (49%)
  starting transfers between devices  122 us (46%)
  waiting for transfers between devices  12.5 us (5%)
    pallas_call x5, Pallas kernels, on_chip(): pl.pallas_call(kernel, out_shape=out_shape, in_specs=[anywhere] * len(in_...  127 us
    ppermute x2, starting transfers between devices, crossed(): return lax.ppermute(block, 'head', [(0, 1), (1, 0)])  113 us
    ppermute x5, waiting for transfers between devices, shifted(): lax.ppermute(block, 'ctx', [(i, (i + distance) % n) for i in range(n)])  7.55 us
  transfers between devices with their start and end apart: 15, of which 8 were waited for; matrix products, arithmetic and copies ran while one was open for 0% of the time, Pallas kernels for 48%

profile of v1, /device:TPU:28, one launch (start us, length us, event | category | flops | bytes accessed | tf_op | source)
XLA Modules:
  0.0 265.0 jit_solution(6420996418625728704)
XLA Ops:
  0.0 1.0 pack.1
  1.0 1.6 collective-permute-start.7
  2.8 1.6 collective-permute-start
  4.4 1.9 collective-permute-done.7.refs_1_
  6.3 2.6 collective-permute-done.6.refs_0_
  9.0 2.1 collective-permute-start.8
  11.1 0.7 collective-permute-done.refs_0_
  11.8 0.7 collective-permute-start.3
  13.5 1.9 collective-permute-done.8.refs_2_.refs_1_
  15.6 1.8 collective-permute-done.3.refs_1_
  17.4 0.8 collective-permute-start.4
  18.8 1.8 collective-permute-done.10.refs_3_.refs_10_.refs_5_
  20.7 0.5 collective-permute-start.2
  21.2 1.2 collective-permute-done.4.refs_2_.refs_5_
  22.4 0.7 join.5
  23.2 1.0 shard_map.46
  24.2 0.7 copy-done
  24.9 3.0 %shard_map.49 = bf16[128,8,128]{2,1,0:T(8,128)(2,1)S(1)} custom-call(bf16[128,8,128]{2,1,0:T(8,128)(2,1)S(1)} %get-tuple-element.14.refs_0_, s32[32,128]{1,0:T(8,128)S(1)} %get-tuple-element.10.refs_1_, bf16[512,128]{1,0:T(8,128)(2,1)S(1)} %get-tuple-element.12.refs_0_.refs_7_.refs_2_, bf16[1024,128]{1,0:T(8,128)(2,1)S(1)} %join.6.refs_8_.refs_3_, ...), custom_call_target="tpu_custom_call" | custom-call | tf_op jit(solution)/shard_map/pallas_call | solution.py:404
  27.9 56.6 %collective-permute-start.14 = (bf16[128,8,128]{2,1,0:T(8,128)(2,1)S(1)}, bf16[128,8,128]{2,1,0:T(8,128)(2,1)S(1)}, u32[]{:S(2)}, u32[]{:S(2)}) collective-permute-start(bf16[128,8,128]{2,1,0:T(8,128)(2,1)S(1)} %shard_map.49), channel_id=1, source_target_pairs={{0,1},{1,0},{2,3},{3,2},{4,5},{5,4},{6,7},{7,6},{8,9},{9,8},{10,11... | collective-permute-start | bytes 786440 | tf_op jit(solution)/shard_map/ppermute | solution.py:35
  84.6 0.9 copy-done.1
  85.5 3.2 %shard_map.48 = bf16[128,8,128]{2,1,0:T(8,128)(2,1)S(1)} custom-call(bf16[128,8,128]{2,1,0:T(8,128)(2,1)S(1)} %copy-done.1, s32[32,128]{1,0:T(8,128)S(1)} %get-tuple-element.10.refs_1_, bf16[512,128]{1,0:T(8,128)(2,1)S(1)} %get-tuple-element.11.refs_0_.refs_2_, bf16[1024,128]{1,0:T(8,128)(2,1)S(1)} %join.4.refs_3_, ...), custom_call_target="tpu_custom_call" | custom-call | tf_op jit(solution)/shard_map/pallas_call | solution.py:404
  88.7 56.1 %collective-permute-start.13 = (bf16[128,8,128]{2,1,0:T(8,128)(2,1)S(1)}, bf16[128,8,128]{2,1,0:T(8,128)(2,1)S(1)}, u32[]{:S(2)}, u32[]{:S(2)}) collective-permute-start(bf16[128,8,128]{2,1,0:T(8,128)(2,1)S(1)} %shard_map.48), channel_id=1, source_target_pairs={{0,1},{1,0},{2,3},{3,2},{4,5},{5,4},{6,7},{7,6},{8,9},{9,8},{10,11... | collective-permute-start | bytes 786440 | tf_op jit(solution)/shard_map/ppermute | solution.py:35
  144.8 119.1 %shard_map.47.out_in = bf16[128,32,128]{2,1,0:T(8,128)(2,1)} custom-call(bf16[256,16,128]{2,1,0:T(8,128)(2,1)} %refs_0_.1, s32[32,128]{1,0:T(8,128)S(1)} %get-tuple-element.10.refs_1_, bf16[512,128]{1,0:T(8,128)(2,1)S(1)} %get-tuple-element.11.refs_0_.refs_2_, bf16[1024,128]{1,0:T(8,128)(2,1)S(1)} %join.4.refs_3_, ...), custom_call_target="tpu_custom_call" | custom-call | tf_op jit(solution)/shard_map/pallas_call | solution.py:404
  264.0 0.8 shard_map.50
  (25 shorter events, 2.3 us)
Async XLA Ops:
  1.0 5.3 %collective-permute-start.7 = (bf16[512,128]{1,0:T(8,128)(2,1)S(1)}, bf16[512,128]{1,0:T(8,128)(2,1)S(1)}, u32[]{:S(2)}, u32[]{:S(2)}) collective-permute-start(bf16[512,128]{1,0:T(8,128)(2,1)S(1)} %get-tuple-element.12.refs_0_.refs_7_.refs_2_), channel_id=1, source_target_pairs={{0,4},{2,6},{4,0},{6,2},{8,12},{10,14},{12,8},{14,10},{16,20},{18,... | collective-permute-start | bytes 393224 | tf_op jit(solution)/shard_map/ppermute | solution.py:31
  2.6 6.4 %collective-permute-start.6 = (bf16[512,128]{1,0:T(8,128)(2,1)S(1)}, bf16[512,128]{1,0:T(8,128)(2,1)S(1)}, u32[]{:S(2)}, u32[]{:S(2)}) collective-permute-start(bf16[512,128]{1,0:T(8,128)(2,1)S(1)} %get-tuple-element.12.refs_0_.refs_7_.refs_2_), channel_id=1, source_target_pairs={{0,8},{2,10},{4,12},{6,14},{8,16},{10,18},{12,20},{14,22},{16,24},... | collective-permute-start | bytes 393224 | tf_op jit(solution)/shard_map/ppermute | solution.py:26
  2.8 9.0 %collective-permute-start = (bf16[512,128]{1,0:T(8,128)(2,1)S(1)}, bf16[512,128]{1,0:T(8,128)(2,1)S(1)}, u32[]{:S(2)}, u32[]{:S(2)}) collective-permute-start(bf16[512,128]{1,0:T(8,128)(2,1)S(1)} %get-tuple-element.11.refs_0_.refs_2_), channel_id=1, source_target_pairs={{0,8},{2,10},{4,12},{6,14},{8,16},{10,18},{12,20},{14,22},{16,24},... | collective-permute-start | bytes 393224 | tf_op jit(solution)/shard_map/ppermute | solution.py:26
  9.0 6.4 %collective-permute-start.8 = (bf16[512,128]{1,0:T(8,128)(2,1)S(1)}, bf16[512,128]{1,0:T(8,128)(2,1)S(1)}, u32[]{:S(2)}, u32[]{:S(2)}) collective-permute-start(bf16[512,128]{1,0:T(8,128)(2,1)S(1)} %broadcast_select_fusion.1), channel_id=1, source_target_pairs={{0,8},{2,10},{4,12},{6,14},{8,16},{10,18},{12,20},{14,22},{16,24},... | collective-permute-start | bytes 393224 | tf_op jit(solution)/shard_map/ppermute | solution.py:26
  11.8 5.6 %collective-permute-start.3 = (bf16[512,128]{1,0:T(8,128)(2,1)S(1)}, bf16[512,128]{1,0:T(8,128)(2,1)S(1)}, u32[]{:S(2)}, u32[]{:S(2)}) collective-permute-start(bf16[512,128]{1,0:T(8,128)(2,1)S(1)} %collective-permute-done.refs_0_), channel_id=1, source_target_pairs={{0,8},{2,10},{4,12},{6,14},{8,16},{10,18},{12,20},{14,22},{16,24},... | collective-permute-start | bytes 393224 | tf_op jit(solution)/shard_map/ppermute | solution.py:26
  12.4 8.2 %collective-permute-start.1 = (bf16[512,128]{1,0:T(8,128)(2,1)S(1)}, bf16[512,128]{1,0:T(8,128)(2,1)S(1)}, u32[]{:S(2)}, u32[]{:S(2)}) collective-permute-start(bf16[512,128]{1,0:T(8,128)(2,1)S(1)} %collective-permute-done.refs_0_), channel_id=1, source_target_pairs={{0,4},{2,6},{4,0},{6,2},{8,12},{10,14},{12,8},{14,10},{16,20},{18,... | collective-permute-start | bytes 393224 | tf_op jit(solution)/shard_map/ppermute | solution.py:31
  13.0 5.8 %collective-permute-start.11 = (bf16[512,128]{1,0:T(8,128)(2,1)S(1)}, bf16[512,128]{1,0:T(8,128)(2,1)S(1)}, u32[]{:S(2)}, u32[]{:S(2)}) collective-permute-start(bf16[512,128]{1,0:T(8,128)(2,1)S(1)} %collective-permute-done.6.refs_0_), channel_id=1, source_target_pairs={{0,8},{2,10},{4,12},{6,14},{8,16},{10,18},{12,20},{14,22},{16,24},... | collective-permute-start | bytes 393224 | tf_op jit(solution)/shard_map/ppermute | solution.py:26
  15.4 5.1 %collective-permute-start.10 = (bf16[512,128]{1,0:T(8,128)(2,1)S(1)}, bf16[512,128]{1,0:T(8,128)(2,1)S(1)}, u32[]{:S(2)}, u32[]{:S(2)}) collective-permute-start(bf16[512,128]{1,0:T(8,128)(2,1)S(1)} %broadcast_select_fusion), channel_id=1, source_target_pairs={{0,4},{2,6},{4,0},{6,2},{8,12},{10,14},{12,8},{14,10},{16,20},{18,... | collective-permute-start | bytes 393224 | tf_op jit(solution)/shard_map/ppermute | solution.py:31
  17.4 5.0 %collective-permute-start.4 = (bf16[512,128]{1,0:T(8,128)(2,1)S(1)}, bf16[512,128]{1,0:T(8,128)(2,1)S(1)}, u32[]{:S(2)}, u32[]{:S(2)}) collective-permute-start(bf16[512,128]{1,0:T(8,128)(2,1)S(1)} %broadcast_select_fusion.2), channel_id=1, source_target_pairs={{0,4},{2,6},{4,0},{6,2},{8,12},{10,14},{12,8},{14,10},{16,20},{18,... | collective-permute-start | bytes 393224 | tf_op jit(solution)/shard_map/ppermute | solution.py:31
  18.2 6.7 %collective-permute-start.9 = (bf16[1024,128]{1,0:T(8,128)(2,1)S(1)}, bf16[1024,128]{1,0:T(8,128)(2,1)S(1)}, u32[]{:S(2)}, u32[]{:S(2)}) collective-permute-start(bf16[1024,128]{1,0:T(8,128)(2,1)S(1)} %join.6.refs_8_.refs_3_), channel_id=1, source_target_pairs={{0,2},{2,0},{4,6},{6,4},{8,10},{10,8},{12,14},{14,12},{16,18},{18,... | collective-permute-start | bytes 786440 | tf_op jit(solution)/shard_map/ppermute | solution.py:31
  20.6 4.3 %collective-permute-start.12 = (bf16[1024,128]{1,0:T(8,128)(2,1)S(1)}, bf16[1024,128]{1,0:T(8,128)(2,1)S(1)}, u32[]{:S(2)}, u32[]{:S(2)}) collective-permute-start(bf16[1024,128]{1,0:T(8,128)(2,1)S(1)} %join.7), channel_id=1, source_target_pairs={{0,2},{2,0},{4,6},{6,4},{8,10},{10,8},{12,14},{14,12},{16,18},{18,... | collective-permute-start | bytes 786440 | tf_op jit(solution)/shard_map/ppermute | solution.py:31
  20.7 2.5 copy-start.2
  20.7 63.8 %collective-permute-start.2 = (bf16[1024,128]{1,0:T(8,128)(2,1)S(1)}, bf16[1024,128]{1,0:T(8,128)(2,1)S(1)}, u32[]{:S(2)}, u32[]{:S(2)}) collective-permute-start(bf16[1024,128]{1,0:T(8,128)(2,1)S(1)} %join.4.refs_3_), channel_id=1, source_target_pairs={{0,2},{2,0},{4,6},{6,4},{8,10},{10,8},{12,14},{14,12},{16,18},{18,... | collective-permute-start | bytes 786440 | tf_op jit(solution)/shard_map/ppermute | solution.py:31
  23.2 61.4 %collective-permute-start.5 = (bf16[1024,128]{1,0:T(8,128)(2,1)}, bf16[1024,128]{1,0:T(8,128)(2,1)S(1)}, u32[]{:S(2)}, u32[]{:S(2)}) collective-permute-start(bf16[1024,128]{1,0:T(8,128)(2,1)} %join.5), channel_id=1, source_target_pairs={{0,2},{2,0},{4,6},{6,4},{8,10},{10,8},{12,14},{14,12},{16,18},{18,... | collective-permute-start | bytes 786440 | tf_op jit(solution)/shard_map/ppermute | solution.py:31
  24.2 0.7 copy-start
  27.9 236.0 %collective-permute-start.14 = (bf16[128,8,128]{2,1,0:T(8,128)(2,1)S(1)}, bf16[128,8,128]{2,1,0:T(8,128)(2,1)S(1)}, u32[]{:S(2)}, u32[]{:S(2)}) collective-permute-start(bf16[128,8,128]{2,1,0:T(8,128)(2,1)S(1)} %shard_map.49), channel_id=1, source_target_pairs={{0,1},{1,0},{2,3},{3,2},{4,5},{5,4},{6,7},{7,6},{8,9},{9,8},{10,11... | collective-permute-start | bytes 786440 | tf_op jit(solution)/shard_map/ppermute | solution.py:35
  84.5 1.0 copy-start.1
  88.7 175.3 %collective-permute-start.13 = (bf16[128,8,128]{2,1,0:T(8,128)(2,1)S(1)}, bf16[128,8,128]{2,1,0:T(8,128)(2,1)S(1)}, u32[]{:S(2)}, u32[]{:S(2)}) collective-permute-start(bf16[128,8,128]{2,1,0:T(8,128)(2,1)S(1)} %shard_map.48), channel_id=1, source_target_pairs={{0,1},{1,0},{2,3},{3,2},{4,5},{5,4},{6,7},{7,6},{8,9},{9,8},{10,11... | collective-permute-start | bytes 786440 | tf_op jit(solution)/shard_map/ppermute | solution.py:35

commit v2 on v1

--- a/solution.py
+++ b/solution.py
@@ -21,9 +21,16 @@
 FLOOR = 2.0**-100
 
 
-def shifted(block, distance):
+def shifted(block, lowest, right_lowest=None):
     n = lax.axis_size("ctx")
-    return lax.ppermute(block, "ctx", [(i, (i + distance) % n) for i in range(n)])
+    last = n // QUAD - 1
+    route = []
+    for i in range(n):
+        plane, place = divmod(i, QUAD)
+        low = lowest if right_lowest is None or place < QUAD // 2 else right_lowest
+        target = plane if plane < low else low if plane == last else plane + 1
+        route.append((i, target * QUAD + place))
+    return lax.ppermute(block, "ctx", route)
 
 
 def swapped(block, bit):
@@ -137,7 +144,7 @@
     return jnp.where(test(lax.axis_index("ctx")), yes, no)
 
 
-def gathered(own, hops, across_first):
+def gathered(own, g, hops, across_first):
     arrays = [own]
     line = own
 
@@ -147,18 +154,18 @@
 
     if across_first:
         beside = swapped(own, 2)
-        line = shifted(own, QUAD)
-        wide = shifted(chosen(left, beside, line), QUAD)
-        back = shifted(line, QUAD)
+        line = shifted(own, 0)
+        wide = shifted(chosen(left, beside, line), 0, 1)
+        back = shifted(line, 1)
         arrays += twin([(None, line)], [(right, beside), (left, wide)])
         across = swapped(chosen(left, line, wide), 2)
         last = [(lower, own), (both(upper, right), wide), (both(upper, left), back)]
     else:
-        for _ in range(1, hops):
-            line = shifted(line, QUAD)
+        for hop in range(1, hops):
+            line = shifted(line, hop - 1)
             across = swapped(line, 2)
             arrays += twin([(None, line)], [(None, across)])
-        line = shifted(line, QUAD)
+        line = shifted(line, hops - 1 if g == 0 else 0)
         across = swapped(chosen(left, own, line), 2)
         last = [(lower, own), (upper, line)]
     return arrays + [across, twin(last, [(None, across)])[1]]
@@ -268,16 +275,25 @@
         copy.wait()
 
 
-def attend_kernel(scale, hops, groups, group, home, *refs):
+def attend_kernel(scale, hops, groups, group, home, aside, *refs):
     refs = list(refs)
     heads = len(groups)
     q_in = refs.pop(0)
+    outside = [refs.pop(0) for _ in aside]
     docs_ref = refs.pop(0)
-    arrays = [[refs.pop(0) for _ in range(2 * hops + 1)] for _ in groups]
+    arrays = [
+        [None if (n, a) in aside else refs.pop(0) for a in range(2 * hops + 1)]
+        for n in range(heads)
+    ]
     out_ref, acc_ref, start_ref, top_ref, p_buf = refs[:5]
     side = lax.axis_index("head")
+    loads = []
     if home:
-        q_ref, piece_ref, sem = refs[5:]
+        q_ref, piece_ref, sem = refs[5:8]
+        for i, (n, a) in enumerate(aside):
+            arrays[n][a] = refs[8 + i]
+            loads.append(pltpu.make_async_copy(outside[i], refs[8 + i], sem.at[heads + i]))
+            loads[i].start()
         half, _, dim = q_ref.shape
         offset = pl.multiple_of(side * half, half)
         q_copy = pltpu.make_async_copy(q_in.at[pl.ds(offset, half)], q_ref, sem.at[0])
@@ -296,6 +312,8 @@
         lows[-1][0] = rows.me * tok
     if home:
         q_copy.wait()
+        for load in loads:
+            load.wait()
     slots = range(len(tables[0]))
     chunks = size // CHUNK
 
@@ -444,10 +462,10 @@
 
     groups, windows, others = [], [], []
     for g in range(kv_heads):
-        groups.append((g, hops == 2 and g % 2 == 1))
-        windows.append(gathered(own[g], hops, groups[g][1]))
+        groups.append((g, False))
+        windows.append(gathered(own[g], g, hops, groups[g][1]))
         away = on_chip(
-            functools.partial(attend_kernel, scale, hops, groups[g : g + 1], group, False),
+            functools.partial(attend_kernel, scale, hops, groups[g : g + 1], group, False, []),
             piece,
             pl.BlockSpec(memory_space=pltpu.VMEM),
             scratch(1),
@@ -455,18 +473,26 @@
             q_away[g], docs, *windows[g],
         )
         others.append(crossed(away))
+    aside = [(0, a) for a in range(2, 2 * hops + 1, 2)] if hops <= NEAR_HOPS else []
+    kept = [
+        array
+        for n, window in enumerate(windows)
+        for a, array in enumerate(window)
+        if (n, a) not in aside
+    ]
     result = on_chip(
-        functools.partial(attend_kernel, scale, hops, groups, group, True),
+        functools.partial(attend_kernel, scale, hops, groups, group, True, aside),
         output,
         anywhere,
         scratch(kv_heads)
         + [
             pltpu.VMEM((half, heads_here, dim), jnp.bfloat16),
             pltpu.VMEM((kv_heads, half, group, dim), jnp.bfloat16),
-            pltpu.SemaphoreType.DMA((kv_heads,)),
-        ],
-        [queries],
-        docs, *[array for window in windows for array in window],
+            pltpu.SemaphoreType.DMA((kv_heads + len(aside),)),
+        ]
+        + [pltpu.VMEM(windows[n][a].shape, jnp.bfloat16) for n, a in aside],
+        [queries] + [windows[n][a] for n, a in aside],
+        docs, *kept,
     )
     return on_chip(
         place_kernel, output, anywhere, [pltpu.SemaphoreType.DMA((kv_heads,))],

time: 265 us -> 266 us (level)
    ppermute x5 -> x4, waiting for transfers between devices: 7.55 us -> 6.62 us  [shifted(): return lax.ppermute(block, 'ctx', route)]
    ppermute x5 -> x4, starting transfers between devices: 5.07 us -> 5.78 us  [shifted(): return lax.ppermute(block, 'ctx', route)]
  transfers between devices with their start and end apart: 15 -> 14, of which waited for: 8 -> 6; matrix products, arithmetic and copies ran while one was open for 0% -> 0% of each run, Pallas kernels for 48% -> 48%
where the time goes in v2:
time: 266 us
  Pallas kernels  130 us (49%)
  starting transfers between devices  124 us (47%)
  waiting for transfers between devices  11.1 us (4%)
    pallas_call x5, Pallas kernels, on_chip(): pl.pallas_call(kernel, out_shape=out_shape, in_specs=[anywhere] * len(in_...  128 us
    ppermute x2, starting transfers between devices, crossed(): return lax.ppermute(block, 'head', [(0, 1), (1, 0)])  113 us
    ppermute x4, waiting for transfers between devices, shifted(): return lax.ppermute(block, 'ctx', route)  6.62 us
    ppermute x8, starting transfers between devices, swapped(): return lax.ppermute(block, 'ctx', [(i, i ^ bit) for i in range(n)])  5.9 us
    ppermute x4, starting transfers between devices, shifted(): return lax.ppermute(block, 'ctx', route)  5.78 us
  transfers between devices with their start and end apart: 14, of which 6 were waited for; matrix products, arithmetic and copies ran while one was open for 0% of the time, Pallas kernels for 48%

profile of v2, /device:TPU:28, one launch (start us, length us, event | category | flops | bytes accessed | tf_op | source)
XLA Modules:
  0.0 266.3 jit_solution(4003992196086549049)
XLA Ops:
  0.0 1.0 pack.1
  1.3 1.6 collective-permute-start
  2.9 4.6 %collective-permute-done.6.refs_0_ = bf16[512,128]{1,0:T(8,128)(2,1)S(1)} collective-permute-done((bf16[512,128]{1,0:T(8,128)(2,1)S(1)}, bf16[512,128]{1,0:T(8,128)(2,1)S(1)}, u32[]{:S(2)}, u32[]{:S(2)}) %collective-permute-start.6) | collective-permute-done | bytes 131104 | tf_op jit(solution)/shard_map/ppermute | solution.py:33
  7.5 2.0 collective-permute-start.9
  9.5 0.8 collective-permute-done.refs_0_
  10.3 1.9 collective-permute-start.3
  12.2 1.6 collective-permute-start.1
  13.7 0.5 collective-permute-start.7
  14.3 1.6 collective-permute-start.10
  15.9 1.3 collective-permute-done.3.refs_1_
  17.1 1.6 collective-permute-start.4
  18.7 2.5 collective-permute-done.7.refs_1_
  21.3 1.3 collective-permute-done.10.refs_2_.refs_10_.refs_5_
  22.7 0.5 collective-permute-start.2
  23.3 0.7 collective-permute-done.4.refs_2_.refs_6_.refs_5_
  24.0 0.7 join.5
  24.7 1.0 shard_map.46
  25.8 0.7 copy-done.2
  26.5 3.7 %shard_map.49 = bf16[128,8,128]{2,1,0:T(8,128)(2,1)} custom-call(bf16[128,8,128]{2,1,0:T(8,128)(2,1)S(1)} %get-tuple-element.14.refs_0_, s32[32,128]{1,0:T(8,128)S(1)} %get-tuple-element.11.refs_3_.refs_1_, bf16[512,128]{1,0:T(8,128)(2,1)S(1)} %get-tuple-element.12.refs_0_.refs_7_.refs_2_, bf16[1024,128]{1,0:T(8,128)(2,1)S(1)} %join.6.refs_8_.refs_3_, ...), custom_call_target="tpu_custom_call" | custom-call | tf_op jit(solution)/shard_map/pallas_call | solution.py:422
  30.2 56.5 %collective-permute-start.13 = (bf16[128,8,128]{2,1,0:T(8,128)(2,1)}, bf16[128,8,128]{2,1,0:T(8,128)(2,1)S(1)}, u32[]{:S(2)}, u32[]{:S(2)}) collective-permute-start(bf16[128,8,128]{2,1,0:T(8,128)(2,1)} %shard_map.49), channel_id=1, source_target_pairs={{0,1},{1,0},{2,3},{3,2},{4,5},{5,4},{6,7},{7,6},{8,9},{9,8},{10,11... | collective-permute-start | bytes 786440 | tf_op jit(solution)/shard_map/ppermute | solution.py:42
  86.7 3.2 %shard_map.48 = bf16[128,8,128]{2,1,0:T(8,128)(2,1)S(1)} custom-call(bf16[128,8,128]{2,1,0:T(8,128)(2,1)S(1)} %copy-done.3, s32[32,128]{1,0:T(8,128)S(1)} %get-tuple-element.11.refs_3_.refs_1_, bf16[512,128]{1,0:T(8,128)(2,1)S(1)} %get-tuple-element.10.refs_0_.refs_4_.refs_2_, bf16[1024,128]{1,0:T(8,128)(2,1)S(1)} %join.4.refs_5_.refs_3_, ...), custom_call_target="tpu_custom_call" | custom-call | tf_op jit(solution)/shard_map/pallas_call | solution.py:422
  90.0 56.1 %collective-permute-start.12 = (bf16[128,8,128]{2,1,0:T(8,128)(2,1)S(1)}, bf16[128,8,128]{2,1,0:T(8,128)(2,1)S(1)}, u32[]{:S(2)}, u32[]{:S(2)}) collective-permute-start(bf16[128,8,128]{2,1,0:T(8,128)(2,1)S(1)} %shard_map.48), channel_id=1, source_target_pairs={{0,1},{1,0},{2,3},{3,2},{4,5},{5,4},{6,7},{7,6},{8,9},{9,8},{10,11... | collective-permute-start | bytes 786440 | tf_op jit(solution)/shard_map/ppermute | solution.py:42
  146.1 119.2 %shard_map.47.out_in = bf16[128,32,128]{2,1,0:T(8,128)(2,1)} custom-call(bf16[256,16,128]{2,1,0:T(8,128)(2,1)} %refs_0_.1, bf16[1024,128]{1,0:T(8,128)(2,1)} %copy-done, bf16[1024,128]{1,0:T(8,128)(2,1)} %copy-done.1, s32[32,128]{1,0:T(8,128)S(1)} %get-tuple-element.11.refs_3_.refs_1_, bf16[512,128]{1,0:T(8,128)(2,1)S(1)} %get-tuple-element.10.refs_0_.refs_4_.refs_2_, ...), custom_call_target="tpu_custom_call" | custom-call | tf_op jit(solution)/shard_map/pallas_call | solution.py:422
  265.3 0.8 shard_map.50
  (26 shorter events, 0.5 us)
Async XLA Ops:
  1.0 6.4 %collective-permute-start.6 = (bf16[512,128]{1,0:T(8,128)(2,1)S(1)}, bf16[512,128]{1,0:T(8,128)(2,1)S(1)}, u32[]{:S(2)}, u32[]{:S(2)}) collective-permute-start(bf16[512,128]{1,0:T(8,128)(2,1)S(1)} %get-tuple-element.12.refs_0_.refs_7_.refs_2_), channel_id=1, source_target_pairs={{0,8},{2,10},{4,12},{6,14},{8,16},{10,18},{12,20},{14,22},{16,24},... | collective-permute-start | bytes 393224 | tf_op jit(solution)/shard_map/ppermute | solution.py:33
  1.3 9.0 %collective-permute-start = (bf16[512,128]{1,0:T(8,128)(2,1)S(1)}, bf16[512,128]{1,0:T(8,128)(2,1)S(1)}, u32[]{:S(2)}, u32[]{:S(2)}) collective-permute-start(bf16[512,128]{1,0:T(8,128)(2,1)S(1)} %get-tuple-element.10.refs_0_.refs_4_.refs_2_), channel_id=1, source_target_pairs={{0,8},{2,10},{4,12},{6,14},{8,16},{10,18},{12,20},{14,22},{16,24},... | collective-permute-start | bytes 393224 | tf_op jit(solution)/shard_map/ppermute | solution.py:33
  7.5 6.8 %collective-permute-start.9 = (bf16[512,128]{1,0:T(8,128)(2,1)S(1)}, bf16[512,128]{1,0:T(8,128)(2,1)S(1)}, u32[]{:S(2)}, u32[]{:S(2)}) collective-permute-start(bf16[512,128]{1,0:T(8,128)(2,1)S(1)} %collective-permute-done.6.refs_0_), channel_id=1, source_target_pairs={{0,8},{2,10},{4,12},{6,14},{8,16},{10,18},{12,20},{14,22},{16,24},... | collective-permute-start | bytes 393224 | tf_op jit(solution)/shard_map/ppermute | solution.py:33
  10.3 6.8 %collective-permute-start.3 = (bf16[512,128]{1,0:T(8,128)(2,1)S(1)}, bf16[512,128]{1,0:T(8,128)(2,1)S(1)}, u32[]{:S(2)}, u32[]{:S(2)}) collective-permute-start(bf16[512,128]{1,0:T(8,128)(2,1)S(1)} %collective-permute-done.refs_0_), channel_id=1, source_target_pairs={{0,0},{2,2},{4,4},{6,6},{8,16},{10,18},{12,20},{14,22},{16,24},{18... | collective-permute-start | bytes 393224 | tf_op jit(solution)/shard_map/ppermute | solution.py:33
  12.2 10.5 %collective-permute-start.1 = (bf16[512,128]{1,0:T(8,128)(2,1)S(1)}, bf16[512,128]{1,0:T(8,128)(2,1)S(1)}, u32[]{:S(2)}, u32[]{:S(2)}) collective-permute-start(bf16[512,128]{1,0:T(8,128)(2,1)S(1)} %collective-permute-done.refs_0_), channel_id=1, source_target_pairs={{0,4},{2,6},{4,0},{6,2},{8,12},{10,14},{12,8},{14,10},{16,20},{18,... | collective-permute-start | bytes 393224 | tf_op jit(solution)/shard_map/ppermute | solution.py:38
  13.7 7.4 %collective-permute-start.7 = (bf16[512,128]{1,0:T(8,128)(2,1)S(1)}, bf16[512,128]{1,0:T(8,128)(2,1)S(1)}, u32[]{:S(2)}, u32[]{:S(2)}) collective-permute-start(bf16[512,128]{1,0:T(8,128)(2,1)S(1)} %collective-permute-done.6.refs_0_), channel_id=1, source_target_pairs={{0,4},{2,6},{4,0},{6,2},{8,12},{10,14},{12,8},{14,10},{16,20},{18,... | collective-permute-start | bytes 393224 | tf_op jit(solution)/shard_map/ppermute | solution.py:38
  14.3 8.3 %collective-permute-start.10 = (bf16[512,128]{1,0:T(8,128)(2,1)S(1)}, bf16[512,128]{1,0:T(8,128)(2,1)S(1)}, u32[]{:S(2)}, u32[]{:S(2)}) collective-permute-start(bf16[512,128]{1,0:T(8,128)(2,1)S(1)} %broadcast_select_fusion), channel_id=1, source_target_pairs={{0,4},{2,6},{4,0},{6,2},{8,12},{10,14},{12,8},{14,10},{16,20},{18,... | collective-permute-start | bytes 393224 | tf_op jit(solution)/shard_map/ppermute | solution.py:38
  17.1 6.8 %collective-permute-start.4 = (bf16[512,128]{1,0:T(8,128)(2,1)S(1)}, bf16[512,128]{1,0:T(8,128)(2,1)S(1)}, u32[]{:S(2)}, u32[]{:S(2)}) collective-permute-start(bf16[512,128]{1,0:T(8,128)(2,1)S(1)} %broadcast_select_fusion.1), channel_id=1, source_target_pairs={{0,4},{2,6},{4,0},{6,2},{8,12},{10,14},{12,8},{14,10},{16,20},{18,... | collective-permute-start | bytes 393224 | tf_op jit(solution)/shard_map/ppermute | solution.py:38
  21.2 5.3 %collective-permute-start.8 = (bf16[1024,128]{1,0:T(8,128)(2,1)S(1)}, bf16[1024,128]{1,0:T(8,128)(2,1)S(1)}, u32[]{:S(2)}, u32[]{:S(2)}) collective-permute-start(bf16[1024,128]{1,0:T(8,128)(2,1)S(1)} %join.6.refs_8_.refs_3_), channel_id=1, source_target_pairs={{0,2},{2,0},{4,6},{6,4},{8,10},{10,8},{12,14},{14,12},{16,18},{18,... | collective-permute-start | bytes 786440 | tf_op jit(solution)/shard_map/ppermute | solution.py:38
  22.6 3.9 %collective-permute-start.11 = (bf16[1024,128]{1,0:T(8,128)(2,1)S(1)}, bf16[1024,128]{1,0:T(8,128)(2,1)S(1)}, u32[]{:S(2)}, u32[]{:S(2)}) collective-permute-start(bf16[1024,128]{1,0:T(8,128)(2,1)S(1)} %join.7), channel_id=1, source_target_pairs={{0,2},{2,0},{4,6},{6,4},{8,10},{10,8},{12,14},{14,12},{16,18},{18,... | collective-permute-start | bytes 786440 | tf_op jit(solution)/shard_map/ppermute | solution.py:38
  22.7 2.0 copy-start.4
  22.7 64.0 %collective-permute-start.2 = (bf16[1024,128]{1,0:T(8,128)(2,1)S(1)}, bf16[1024,128]{1,0:T(8,128)(2,1)S(1)}, u32[]{:S(2)}, u32[]{:S(2)}) collective-permute-start(bf16[1024,128]{1,0:T(8,128)(2,1)S(1)} %join.4.refs_5_.refs_3_), channel_id=1, source_target_pairs={{0,2},{2,0},{4,6},{6,4},{8,10},{10,8},{12,14},{14,12},{16,18},{18,... | collective-permute-start | bytes 786440 | tf_op jit(solution)/shard_map/ppermute | solution.py:38
  24.7 62.0 %collective-permute-start.5 = (bf16[1024,128]{1,0:T(8,128)(2,1)}, bf16[1024,128]{1,0:T(8,128)(2,1)S(1)}, u32[]{:S(2)}, u32[]{:S(2)}) collective-permute-start(bf16[1024,128]{1,0:T(8,128)(2,1)} %join.5), channel_id=1, source_target_pairs={{0,2},{2,0},{4,6},{6,4},{8,10},{10,8},{12,14},{14,12},{16,18},{18,... | collective-permute-start | bytes 786440 | tf_op jit(solution)/shard_map/ppermute | solution.py:38
  25.8 0.7 copy-start.2
  26.5 60.3 %copy-start.3 = (bf16[128,8,128]{2,1,0:T(8,128)(2,1)S(1)}, bf16[128,8,128]{2,1,0:T(8,128)(2,1)}, u32[]{:S(2)}) copy-start(bf16[128,8,128]{2,1,0:T(8,128)(2,1)} %copy-done.2) | copy-start | bytes 786436
  30.2 235.1 %collective-permute-start.13 = (bf16[128,8,128]{2,1,0:T(8,128)(2,1)}, bf16[128,8,128]{2,1,0:T(8,128)(2,1)S(1)}, u32[]{:S(2)}, u32[]{:S(2)}) collective-permute-start(bf16[128,8,128]{2,1,0:T(8,128)(2,1)} %shard_map.49), channel_id=1, source_target_pairs={{0,1},{1,0},{2,3},{3,2},{4,5},{5,4},{6,7},{7,6},{8,9},{9,8},{10,11... | collective-permute-start | bytes 786440 | tf_op jit(solution)/shard_map/ppermute | solution.py:42
  86.7 3.2 %copy-start = (bf16[1024,128]{1,0:T(8,128)(2,1)}, bf16[1024,128]{1,0:T(8,128)(2,1)S(1)}, u32[]{:S(2)}) copy-start(bf16[1024,128]{1,0:T(8,128)(2,1)S(1)} %collective-permute-done.2.refs_1_.refs_4_) | copy-start | bytes 786436
  86.7 3.2 %copy-start.1 = (bf16[1024,128]{1,0:T(8,128)(2,1)}, bf16[1024,128]{1,0:T(8,128)(2,1)S(1)}, u32[]{:S(2)}) copy-start(bf16[1024,128]{1,0:T(8,128)(2,1)S(1)} %collective-permute-done.5.refs_2_.refs_6_) | copy-start | bytes 786436
  90.0 175.3 %collective-permute-start.12 = (bf16[128,8,128]{2,1,0:T(8,128)(2,1)S(1)}, bf16[128,8,128]{2,1,0:T(8,128)(2,1)S(1)}, u32[]{:S(2)}, u32[]{:S(2)}) collective-permute-start(bf16[128,8,128]{2,1,0:T(8,128)(2,1)S(1)} %shard_map.48), channel_id=1, source_target_pairs={{0,1},{1,0},{2,3},{3,2},{4,5},{5,4},{6,7},{7,6},{8,9},{9,8},{10,11... | collective-permute-start | bytes 786440 | tf_op jit(solution)/shard_map/ppermute | solution.py:42
